TPU v7x, 32 devices: a whole 2x2x4 slice. The times are simulated.
32 devices in a mesh: data: 2 (over x), col: 4 (over z), row: 4 (over y, core).
Axes of the slice: x: 2, y: 2, z: 4, core: 2. Of those that a mesh axis runs over, the one named last changes fastest.
Arguments:
- x: bfloat16 [16, 64, 4096], P(None, 'data', 'row'), parts along dimension 1
- w_x1: bfloat16 [2, 4096, 16384], P(None, 'row', 'col')
- w_h1: bfloat16 [2, 4096, 16384], P(None, 'row', 'col')
- b_1: float32 [2, 16384], P(None, 'col')
- w_x2: bfloat16 [2, 4096, 16384], P(None, 'row', 'col')
- w_h2: bfloat16 [4096, 16384], P('row', 'col')
- b_2: float32 [16384], P('col')
- h_zero: float32 [3, 64, 4096], P(None, 'data', 'row'), parts along dimension 1
- c_zero: float32 [3, 64, 4096], P(None, 'data', 'row'), parts along dimension 1
Outputs:
- output 1: bfloat16 [16, 64, 4096], P(None, 'data', ('col', 'row')), parts along dimension 1
- output 2: float32 [3, 64, 4096], P(None, 'data', ('col', 'row')), parts along dimension 1
There are 2 independent parts. A program takes and returns all parts, laid end to end along the dimension named above; an argument that names none is the same for every part.
All inputs are finite; a program needn't handle non-finite values.
Results may differ from a plain program's by a relative error of at most 0.00315333.
Values are sent between devices in bfloat16 or wider.
A program may use at most 1 GiB of HBM per device.

v0:
```python
import jax
import jax.numpy as jnp
from jax import lax
from jax.sharding import PartitionSpec as P


def lstm_sweep(in_seq, w_in, w_rec, gate_bias, h_rows, c_own, backward, emit_rows, row_idx):
    d_row = h_rows.shape[-1]

    def one_step(carry, in_t):
        h_prev, c_prev = carry
        part_z = (jnp.dot(in_t, w_in, preferred_element_type=jnp.float32)
                  + jnp.dot(h_prev, w_rec, preferred_element_type=jnp.float32))
        z_own = lax.psum_scatter(part_z, 'row', scatter_dimension=1, tiled=True) + gate_bias
        gates = z_own.reshape(z_own.shape[0], -1, 4)
        c_next = (jax.nn.sigmoid(gates[:, :, 1]) * c_prev
                  + jax.nn.sigmoid(gates[:, :, 0]) * jnp.tanh(gates[:, :, 2]))
        h_own = (jax.nn.sigmoid(gates[:, :, 3]) * jnp.tanh(c_next)).astype(jnp.bfloat16)
        h_cols = lax.all_gather(h_own, 'row', axis=1, tiled=True)
        h_full = lax.all_gather(h_cols, 'col', axis=1, tiled=True)
        h_next = lax.dynamic_slice_in_dim(h_full, row_idx * d_row, d_row, axis=1)
        return (h_next, c_next), (h_next if emit_rows else h_own)

    carry_out, emitted = lax.scan(one_step, (h_rows, c_own), in_seq, reverse=backward)
    return emitted, carry_out[1]


def solution(mesh):
    n_row = mesh.shape['row']
    n_col = mesh.shape['col']
    spec_seq = P(None, 'data', 'row')
    spec_weight = P(None, 'row', 'col')
    spec_out = P(None, 'data', ('col', 'row'))

    def local(x_rows, w_x1, w_h1, b_1, w_x2, w_h2, b_2, h_zero, c_zero):
        row_idx = lax.axis_index('row')
        col_idx = lax.axis_index('col')
        d_row = x_rows.shape[-1]
        unit_n = d_row // n_col
        own_start = col_idx * (unit_n * n_row) + row_idx * unit_n
        bias_one = lax.dynamic_slice_in_dim(b_1, row_idx * 4 * unit_n, 4 * unit_n, axis=1)
        bias_two = lax.dynamic_slice_in_dim(b_2, row_idx * 4 * unit_n, 4 * unit_n, axis=0)
        c_full = lax.all_gather(c_zero, 'row', axis=2, tiled=True)
        c_own = lax.dynamic_slice_in_dim(c_full, own_start, unit_n, axis=2)
        h_rows = h_zero.astype(jnp.bfloat16)
        fwd_rows, fwd_cell = lstm_sweep(x_rows, w_x1[0], w_h1[0], bias_one[0], h_rows[0], c_own[0],
                                        False, True, row_idx)
        bwd_rows, bwd_cell = lstm_sweep(x_rows, w_x1[1], w_h1[1], bias_one[1], h_rows[1], c_own[1],
                                        True, True, row_idx)
        mid_rows = jnp.concatenate([fwd_rows, bwd_rows], axis=2)
        w_mid = w_x2.reshape(2 * d_row, w_x2.shape[2])
        top_own, top_cell = lstm_sweep(mid_rows, w_mid, w_h2, bias_two, h_rows[2], c_own[2],
                                       False, False, row_idx)
        return top_own, jnp.stack([fwd_cell, bwd_cell, top_cell])

    return jax.shard_map(local, mesh=mesh,
                         in_specs=(spec_seq, spec_weight, spec_weight, P(None, 'col'), spec_weight,
                                   P('row', 'col'), P('col'), spec_seq, spec_seq),
                         out_specs=(spec_out, spec_out), check_vma=False)
```

profile of v0, /device:TPU:0, one launch (start us, length us, event | category | flops | bytes accessed | tf_op | source)
XLA Modules:
  0.0 2582.8 jit_solution(17635951355983392523)
XLA Ops:
  9.8 22.9 slice_bitcast_fusion.2
  33.7 828.5 %while.50 = (s32[]{:T(128)}, bf16[32,1024]{1,0:T(8,128)(2,1)S(1)}, f32[32,256]{1,0:T(8,128)S(1)}, bf16[16,32,1024]{2,1,0:T(8,128)(2,1)S(1)}, bf16[16,32,1024]{2,...) while((s32[]{:T(128)}, bf16[32,1024]{1,0:T(8,128)(2,1)S(1)}, ...), condition=%wide.region_2.3_spmd, body=%wide.region_0.2_spmd.sunk | while | flops 537149440 | bytes 47485136 | solution.py:24
  42.0 24.5 reduce-scatter.4.cloned.1.call-done
  95.8 22.3 reduce-scatter.4.cloned.1.call-done
  199.1 22.3 reduce-scatter.4.cloned.1.call-done
  250.7 22.3 reduce-scatter.4.cloned.1.call-done
  302.4 22.3 reduce-scatter.4.cloned.1.call-done
  354.0 22.3 reduce-scatter.4.cloned.1.call-done
  405.7 22.3 reduce-scatter.4.cloned.1.call-done
  560.5 22.3 reduce-scatter.4.cloned.1.call-done
  612.2 22.3 reduce-scatter.4.cloned.1.call-done
  663.8 22.3 reduce-scatter.4.cloned.1.call-done
  715.5 22.3 reduce-scatter.4.cloned.1.call-done
  767.1 22.3 reduce-scatter.4.cloned.1.call-done
  862.3 826.7 %while.51 = (s32[]{:T(128)}, bf16[32,1024]{1,0:T(8,128)(2,1)S(1)}, f32[32,256]{1,0:T(8,128)S(1)}, bf16[16,32,1024]{2,1,0:T(8,128)(2,1)S(1)}, bf16[16,32,1024]{2,...) while((s32[]{:T(128)}, bf16[32,1024]{1,0:T(8,128)(2,1)S(1)}, ...), condition=%wide.region_5.6_spmd, body=%wide.region_3.5_spmd.sunk | while | flops 537149440 | bytes 47485148 | solution.py:24
  974.0 22.3 reduce-scatter.6.cloned.1.call-done
  1025.6 22.3 reduce-scatter.6.cloned.1.call-done
  1129.0 22.3 reduce-scatter.6.cloned.1.call-done
  1284.0 22.3 reduce-scatter.6.cloned.1.call-done
  1439.0 22.3 reduce-scatter.6.cloned.1.call-done
  1594.0 22.3 reduce-scatter.6.cloned.1.call-done
  1690.5 884.8 %while.52 = (s32[]{:T(128)}, bf16[32,1024]{1,0:T(8,128)(2,1)S(1)}, f32[32,256]{1,0:T(8,128)S(1)}, bf16[16,32,256]{2,1,0:T(8,128)(2,1)}, bf16[16,32,2048]{2,1,0:T...) while((s32[]{:T(128)}, bf16[32,1024]{1,0:T(8,128)(2,1)S(1)}, ...), condition=%wide.region_8.9_spmd, body=%wide.region_6.8_spmd.sunk | while | flops 805584896 | bytes 64278716 | solution.py:24
  1701.9 22.3 reduce-scatter.8.cloned.1.call-done
  2365.5 22.3 reduce-scatter.8.cloned.1.call-done
  (954 shorter events, 2093.7 us)
Async XLA Ops:
  33.7 32.8 %reduce-scatter.4.cloned.1.call-start = ((), (), s32[]{:S(2)}) async-start(), calls=%async_computation.4 | async-start | bytes 655360 | tf_op jit(solution)/shard_map/while/body/eval_jaxpr/reduce_scatter | solution.py:14
  294.1 30.6 %reduce-scatter.4.cloned.1.call-start = ((), (), s32[]{:S(2)}) async-start(), calls=%async_computation.4 | async-start | bytes 655360 | tf_op jit(solution)/shard_map/while/body/eval_jaxpr/reduce_scatter | solution.py:14
  345.7 30.6 %reduce-scatter.4.cloned.1.call-start = ((), (), s32[]{:S(2)}) async-start(), calls=%async_computation.4 | async-start | bytes 655360 | tf_op jit(solution)/shard_map/while/body/eval_jaxpr/reduce_scatter | solution.py:14
  965.6 30.6 %reduce-scatter.6.cloned.1.call-start = ((), (), s32[]{:S(2)}) async-start(), calls=%async_computation.5 | async-start | bytes 655360 | tf_op jit(solution)/shard_map/while/body/eval_jaxpr/reduce_scatter | solution.py:14
  1120.6 30.6 %reduce-scatter.6.cloned.1.call-start = ((), (), s32[]{:S(2)}) async-start(), calls=%async_computation.5 | async-start | bytes 655360 | tf_op jit(solution)/shard_map/while/body/eval_jaxpr/reduce_scatter | solution.py:14
  1275.6 30.6 %reduce-scatter.6.cloned.1.call-start = ((), (), s32[]{:S(2)}) async-start(), calls=%async_computation.5 | async-start | bytes 655360 | tf_op jit(solution)/shard_map/while/body/eval_jaxpr/reduce_scatter | solution.py:14
  1430.7 30.6 %reduce-scatter.6.cloned.1.call-start = ((), (), s32[]{:S(2)}) async-start(), calls=%async_computation.5 | async-start | bytes 655360 | tf_op jit(solution)/shard_map/while/body/eval_jaxpr/reduce_scatter | solution.py:14
  1585.7 30.6 %reduce-scatter.6.cloned.1.call-start = ((), (), s32[]{:S(2)}) async-start(), calls=%async_computation.5 | async-start | bytes 655360 | tf_op jit(solution)/shard_map/while/body/eval_jaxpr/reduce_scatter | solution.py:14
  1690.5 33.7 %reduce-scatter.8.cloned.1.call-start = ((), (), s32[]{:S(2)}) async-start(), calls=%async_computation.6 | async-start | bytes 655360 | tf_op jit(solution)/shard_map/while/body/eval_jaxpr/reduce_scatter | solution.py:14
  1745.8 33.7 %reduce-scatter.8.cloned.1.call-start = ((), (), s32[]{:S(2)}) async-start(), calls=%async_computation.6 | async-start | bytes 655360 | tf_op jit(solution)/shard_map/while/body/eval_jaxpr/reduce_scatter | solution.py:14
  1801.1 33.7 %reduce-scatter.8.cloned.1.call-start = ((), (), s32[]{:S(2)}) async-start(), calls=%async_computation.6 | async-start | bytes 655360 | tf_op jit(solution)/shard_map/while/body/eval_jaxpr/reduce_scatter | solution.py:14
  1856.4 33.7 %reduce-scatter.8.cloned.1.call-start = ((), (), s32[]{:S(2)}) async-start(), calls=%async_computation.6 | async-start | bytes 655360 | tf_op jit(solution)/shard_map/while/body/eval_jaxpr/reduce_scatter | solution.py:14
  1911.7 33.7 %reduce-scatter.8.cloned.1.call-start = ((), (), s32[]{:S(2)}) async-start(), calls=%async_computation.6 | async-start | bytes 655360 | tf_op jit(solution)/shard_map/while/body/eval_jaxpr/reduce_scatter | solution.py:14
  1967.0 33.7 %reduce-scatter.8.cloned.1.call-start = ((), (), s32[]{:S(2)}) async-start(), calls=%async_computation.6 | async-start | bytes 655360 | tf_op jit(solution)/shard_map/while/body/eval_jaxpr/reduce_scatter | solution.py:14
  2022.3 33.7 %reduce-scatter.8.cloned.1.call-start = ((), (), s32[]{:S(2)}) async-start(), calls=%async_computation.6 | async-start | bytes 655360 | tf_op jit(solution)/shard_map/while/body/eval_jaxpr/reduce_scatter | solution.py:14
  2077.6 33.7 %reduce-scatter.8.cloned.1.call-start = ((), (), s32[]{:S(2)}) async-start(), calls=%async_computation.6 | async-start | bytes 655360 | tf_op jit(solution)/shard_map/while/body/eval_jaxpr/reduce_scatter | solution.py:14
  2132.9 33.7 %reduce-scatter.8.cloned.1.call-start = ((), (), s32[]{:S(2)}) async-start(), calls=%async_computation.6 | async-start | bytes 655360 | tf_op jit(solution)/shard_map/while/body/eval_jaxpr/reduce_scatter | solution.py:14
  2188.2 33.7 %reduce-scatter.8.cloned.1.call-start = ((), (), s32[]{:S(2)}) async-start(), calls=%async_computation.6 | async-start | bytes 655360 | tf_op jit(solution)/shard_map/while/body/eval_jaxpr/reduce_scatter | solution.py:14
  2243.5 33.7 %reduce-scatter.8.cloned.1.call-start = ((), (), s32[]{:S(2)}) async-start(), calls=%async_computation.6 | async-start | bytes 655360 | tf_op jit(solution)/shard_map/while/body/eval_jaxpr/reduce_scatter | solution.py:14
  2298.8 33.7 %reduce-scatter.8.cloned.1.call-start = ((), (), s32[]{:S(2)}) async-start(), calls=%async_computation.6 | async-start | bytes 655360 | tf_op jit(solution)/shard_map/while/body/eval_jaxpr/reduce_scatter | solution.py:14
  2354.1 33.7 %reduce-scatter.8.cloned.1.call-start = ((), (), s32[]{:S(2)}) async-start(), calls=%async_computation.6 | async-start | bytes 655360 | tf_op jit(solution)/shard_map/while/body/eval_jaxpr/reduce_scatter | solution.py:14
  2409.4 33.7 %reduce-scatter.8.cloned.1.call-start = ((), (), s32[]{:S(2)}) async-start(), calls=%async_computation.6 | async-start | bytes 655360 | tf_op jit(solution)/shard_map/while/body/eval_jaxpr/reduce_scatter | solution.py:14
  2464.7 33.7 %reduce-scatter.8.cloned.1.call-start = ((), (), s32[]{:S(2)}) async-start(), calls=%async_computation.6 | async-start | bytes 655360 | tf_op jit(solution)/shard_map/while/body/eval_jaxpr/reduce_scatter | solution.py:14
  2520.0 33.7 %reduce-scatter.8.cloned.1.call-start = ((), (), s32[]{:S(2)}) async-start(), calls=%async_computation.6 | async-start | bytes 655360 | tf_op jit(solution)/shard_map/while/body/eval_jaxpr/reduce_scatter | solution.py:14
  (106 other events, 2085.1 us)
Sparse Core Ops, SparseCore 0:
  9.5 22.1 all-gather.1
  42.1 24.2 reduce-scatter.3
  95.9 22.1 reduce-scatter.3
  199.2 22.1 reduce-scatter.3
  250.9 22.1 reduce-scatter.3
  302.5 22.1 reduce-scatter.3
  354.1 22.1 reduce-scatter.3
  405.8 22.1 reduce-scatter.3
  560.6 22.1 reduce-scatter.3
  612.3 22.1 reduce-scatter.3
  664.0 22.1 reduce-scatter.3
  715.6 22.1 reduce-scatter.3
  767.3 22.1 reduce-scatter.3
  818.9 22.1 reduce-scatter.3
  870.7 22.1 reduce-scatter.5
  922.4 22.1 reduce-scatter.5
  974.1 22.1 reduce-scatter.5
  1025.7 22.1 reduce-scatter.5
  1129.1 22.1 reduce-scatter.5
  1284.1 22.1 reduce-scatter.5
  1439.1 22.1 reduce-scatter.5
  1594.1 22.1 reduce-scatter.5
  1702.0 22.1 reduce-scatter.7
  2365.6 22.1 reduce-scatter.7
  (25 shorter events, 551.6 us)
where the time goes:
time: 2580 us
  waiting for transfers between devices  1070 us (41%)
  blocking collectives  918 us (36%)
  matrix products  420 us (16%)
  local copies, waits for them, and re-layouts  90.7 us (4%)
  other arithmetic  60 us (2%)
    reduce_scatter x48, waiting for transfers between devices, one_step(): lax.psum_scatter(part_z, 'row', scatter_dimension=1, tiled=True) + gate_bias  1070 us
    all_gather x48, blocking collectives, one_step(): h_full = lax.all_gather(h_cols, 'col', axis=1, tiled=True)  667 us
    dot_general x48, matrix products, one_step(): jnp.dot(in_t, w_in, preferred_element_type=jnp.float32)  307 us
    all_gather x48, blocking collectives, one_step(): h_cols = lax.all_gather(h_own, 'row', axis=1, tiled=True)  251 us
    dot_general x48, matrix products, one_step(): jnp.dot(h_prev, w_rec, preferred_element_type=jnp.float32)  113 us
  transfers between devices with their start and end apart: 49, of which 48 were waited for; matrix products, arithmetic and copies ran while one was open for 1% of the time, Pallas kernels for 0%

commit v1 on v0

v1 whole, which is shorter than its diff:
```python
import functools

import jax
import jax.numpy as jnp
from jax import lax
from jax.experimental import pallas as pl
from jax.experimental.pallas import tpu as pltpu
from jax.sharding import PartitionSpec as P

MESH = pl.DeviceIdType.MESH
F32 = jnp.float32
BF16 = jnp.bfloat16
LANES = 128


def lstm_kernel(steps, n_row, n_col,
                x_ref, wx1_hbm, wh1_hbm, wx2_hbm, wh2_hbm, b1_ref, b2_ref, h0_ref, c0_ref,
                out_ref, c_ref,
                wx, wh, wh2, hist, h2b, zp, p1r, yr, hsend, sel,
                w_sem, p1_send, p1_recv, y_send, y_recv, h_send, h_recv):
    row = lax.axis_index('row')
    col = lax.axis_index('col')
    batch, d_row = x_ref.shape[1], x_ref.shape[2]
    unit_n = d_row // n_col
    width = 4 * unit_n
    core = row % 2
    mate = row + 1 - 2 * core
    across = (row + 2) % 4
    order = (3 - row, across, mate, row)

    def weight_copy(src, dst, idx, sem):
        cols = pl.ds(pl.multiple_of(order[idx] * width, LANES), width)
        return pltpu.make_async_copy(src.at[:, cols], dst.at[idx], w_sem.at[sem, idx])

    loads = {'x0': (wx1_hbm.at[0], wx.at[0], 0), 'h0': (wh1_hbm.at[0], wh.at[0], 1),
             'x1': (wx1_hbm.at[1], wx.at[1], 2), 'h1': (wh1_hbm.at[1], wh.at[1], 3),
             'h2': (wh2_hbm, wh2, 4),
             'm0': (wx2_hbm.at[0], wx.at[0], 5), 'm1': (wx2_hbm.at[1], wx.at[1], 6)}

    def load_start(name):
        for idx in range(4):
            src, dst, sem = loads[name]
            weight_copy(src, dst, idx, sem).start()

    def load_wait(name):
        for idx in range(4):
            src, dst, sem = loads[name]
            weight_copy(src, dst, idx, sem).wait()

    for name in ('x0', 'h0', 'x1', 'h1', 'h2'):
        load_start(name)

    barrier = pltpu.get_barrier_semaphore()
    for dc in range(n_col):
        for dr in range(n_row):
            if dc or dr:
                pl.semaphore_signal(barrier, inc=1, device_id_type=MESH,
                                    device_id={'col': (col + dc) % n_col, 'row': (row + dr) % n_row})

    rr = lax.broadcasted_iota(jnp.int32, (width, unit_n), 0)
    cc = lax.broadcasted_iota(jnp.int32, (width, unit_n), 1)
    sel[...] = jnp.where(rr == 4 * cc, 1.0, 0.0).astype(BF16)
    for k in range(2):
        for j in range(n_row):
            hist[k, 0, j] = h0_ref[k, :, j * unit_n:(j + 1) * unit_n].astype(BF16)
    for j in range(n_row):
        h2b[0, j] = h0_ref[2, :, j * unit_n:(j + 1) * unit_n].astype(BF16)
    c_ref[...] = c0_ref[...]

    def dot(a, w):
        return jnp.dot(a, w, preferred_element_type=F32)

    def joined(blocks):
        return jnp.concatenate([blocks[j] for j in range(n_row)], axis=1)

    def input_product(k, t):
        a = x_ref[t]
        for idx in range(4):
            zp[k, idx] = dot(a, wx[k, idx])

    load_wait('x0')
    input_product(0, 0)
    load_wait('x1')
    input_product(1, steps - 1)
    load_wait('h0')
    load_wait('h1')
    pl.semaphore_wait(barrier, n_col * n_row - 1)

    def mate_copy(k, slot, part):
        return pltpu.make_async_remote_copy(
            src_ref=zp.at[k, 2 * part], dst_ref=p1r.at[k, slot, part],
            send_sem=p1_send.at[k, part], recv_sem=p1_recv.at[k, slot, part],
            device_id={'row': mate}, device_id_type=MESH)

    def across_copy(k, slot):
        return pltpu.make_async_remote_copy(
            src_ref=zp.at[k, 1], dst_ref=yr.at[k, slot],
            send_sem=y_send.at[k], recv_sem=y_recv.at[k, slot],
            device_id={'row': across}, device_id_type=MESH)

    def h_copy(k, dst, slot, i):
        return pltpu.make_async_remote_copy(
            src_ref=hsend.at[k], dst_ref=dst.at[row],
            send_sem=h_send.at[k, i], recv_sem=h_recv.at[k, slot, row],
            device_id={'col': (col + i) % n_col, 'row': col}, device_id_type=MESH)

    own_stays = row == col

    def h_start(k, dst, slot):
        for i in range(n_col - 1, 0, -1):
            h_copy(k, dst, slot, i).start()

        @pl.when(jnp.logical_not(own_stays))
        def _():
            h_copy(k, dst, slot, 0).start()

        @pl.when(own_stays)
        def _():
            dst[row] = hsend[k]

    def h_wait_send(k, dst, slot):
        for i in range(1, n_col):
            h_copy(k, dst, slot, i).wait_send()

        @pl.when(jnp.logical_not(own_stays))
        def _():
            h_copy(k, dst, slot, 0).wait_send()

    def h_wait_recv(k, dst, slot):
        for j in range(n_row):
            def wait(j=j):
                pltpu.make_async_remote_copy(
                    src_ref=hsend.at[k], dst_ref=dst.at[j],
                    send_sem=h_send.at[k, 0], recv_sem=h_recv.at[k, slot, j],
                    device_id={'col': col, 'row': row}, device_id_type=MESH).wait_recv()
            pl.when(jnp.logical_not(own_stays & (row == j)))(wait)

    def head(k, slot, blocks, w_rec):
        a = joined(blocks)
        for idx in range(4):
            zp[k, idx] = zp[k, idx] + dot(a, w_rec[idx])
            if idx % 2 == 0:
                mate_copy(k, slot, idx // 2).start()

    def middle(k, slot):
        mate_copy(k, slot, 0).wait_recv()
        zp[k, 1] = zp[k, 1] + p1r[k, slot, 0]
        across_copy(k, slot).start()

    def gates(k, slot, cell, bias_ref, bias_row):
        mate_copy(k, slot, 1).wait_recv()
        across_copy(k, slot).wait_recv()
        gate = lax.broadcasted_iota(jnp.int32, (batch, LANES), 1) % 4
        scale = jnp.where(gate == 2, 1.0, 0.5)
        shift = jnp.where(gate == 2, 0.0, 0.5)
        pieces = []
        for p in range(width // LANES):
            lanes = slice(p * LANES, (p + 1) * LANES)
            bias = bias_ref[bias_row:bias_row + 1, pl.ds(pl.multiple_of(row * width, LANES) + p * LANES, LANES)]
            z = zp[k, 3, :, lanes] + p1r[k, slot, 1, :, lanes] + yr[k, slot, :, lanes] + bias
            act = jnp.tanh(z * scale) * scale + shift
            f = pltpu.roll(act, LANES - 1, 1)
            g = pltpu.roll(act, LANES - 2, 1)
            o = pltpu.roll(act, LANES - 3, 1)
            c_new = f * c_ref[cell, :, lanes] + act * g
            c_ref[cell, :, lanes] = c_new
            pieces.append((o * jnp.tanh(c_new)).astype(BF16))
        h = dot(jnp.concatenate(pieces, axis=1), sel[...]).astype(BF16)
        for part in range(2):
            mate_copy(k, slot, part).wait_send()
        across_copy(k, slot).wait_send()
        return h

    def layer_one(n, carry):
        slot = n % 2
        for k in range(2):
            @pl.when(n > 0)
            def _(k=k):
                h_wait_recv(k, hist.at[k, n], slot)
            head(k, slot, hist.at[k, n], wh.at[k])
            middle(k, slot)
        for k in range(2):
            h = gates(k, slot, k, b1_ref, k)

            @pl.when(n > 0)
            def _(k=k):
                h_wait_send(k, hist.at[k, n], slot)
            hsend[k] = h
            h_start(k, hist.at[k, n + 1], (n + 1) % 2)

            @pl.when(n < steps - 1)
            def _(k=k):
                input_product(k, n + 1 if k == 0 else steps - 2 - n)

            @pl.when(n == steps - 1)
            def _(k=k):
                load_start('m0' if k == 0 else 'm1')
        return carry

    lax.fori_loop(0, steps, layer_one, 0)

    def mid_product(t):
        a = joined(hist.at[0, t + 1])
        b = joined(hist.at[1, steps - t])
        for idx in range(4):
            zp[0, idx] = dot(a, wx[0, idx]) + dot(b, wx[1, idx])

    for k in range(2):
        h_wait_send(k, hist.at[k, steps], steps % 2)
    for name in ('h2', 'm0', 'm1'):
        load_wait(name)
    for k in range(2):
        h_wait_recv(k, hist.at[k, steps], steps % 2)
    mid_product(0)

    def layer_two(n, carry):
        slot = n % 2

        @pl.when(n > 0)
        def _():
            h_wait_recv(2, h2b.at[slot], slot)
        head(0, slot, h2b.at[slot], wh2)
        middle(0, slot)
        h = gates(0, slot, 2, b2_ref, 0)

        @pl.when(n > 0)
        def _():
            h_wait_send(2, h2b.at[slot], slot)
        hsend[2] = h
        out_ref[n] = h

        @pl.when(n < steps - 1)
        def _():
            h_start(2, h2b.at[1 - slot], 1 - slot)
            mid_product(n + 1)
        return carry

    lax.fori_loop(0, steps, layer_two, 0)


def solution(mesh):
    n_row = mesh.shape['row']
    n_col = mesh.shape['col']
    spec_seq = P(None, 'data', 'row')
    spec_weight = P(None, 'row', 'col')
    spec_out = P(None, 'data', ('col', 'row'))

    def local(x_rows, w_x1, w_h1, b_1, w_x2, w_h2, b_2, h_zero, c_zero):
        row_idx = lax.axis_index('row')
        col_idx = lax.axis_index('col')
        steps, batch, d_row = x_rows.shape
        unit_n = d_row // n_col
        width = 4 * unit_n
        c_part = lax.dynamic_slice_in_dim(c_zero, col_idx * unit_n, unit_n, axis=2)
        pairs = [(b * n_row + a, a * n_row + b) for a in range(n_row) for b in range(n_col)]
        c_own = lax.ppermute(c_part, ('col', 'row'), pairs)
        c_wide = jnp.repeat(c_own, 4, axis=2)
        vmem = pl.BlockSpec(memory_space=pltpu.VMEM)
        hbm = pl.BlockSpec(memory_space=pl.ANY)
        dma = pltpu.SemaphoreType.DMA
        out, c_out = pl.pallas_call(
            functools.partial(lstm_kernel, steps, n_row, n_col),
            out_shape=(jax.ShapeDtypeStruct((steps, batch, unit_n), BF16),
                       jax.ShapeDtypeStruct((3, batch, width), F32)),
            in_specs=[vmem, hbm, hbm, hbm, hbm, vmem, vmem, vmem, vmem],
            out_specs=(vmem, vmem),
            scratch_shapes=[
                pltpu.VMEM((2, 4, d_row, width), BF16),
                pltpu.VMEM((2, 4, d_row, width), BF16),
                pltpu.VMEM((4, d_row, width), BF16),
                pltpu.VMEM((2, steps + 1, n_row, batch, unit_n), BF16),
                pltpu.VMEM((2, n_row, batch, unit_n), BF16),
                pltpu.VMEM((2, 4, batch, width), F32),
                pltpu.VMEM((2, 2, 2, batch, width), F32),
                pltpu.VMEM((2, 2, batch, width), F32),
                pltpu.VMEM((3, batch, unit_n), BF16),
                pltpu.VMEM((width, unit_n), BF16),
                dma((7, 4)), dma((2, 2)), dma((2, 2, 2)), dma((2,)), dma((2, 2)),
                dma((3, n_col)), dma((3, 2, n_row)),
            ],
            compiler_params=pltpu.CompilerParams(
                collective_id=0, has_side_effects=True, vmem_limit_bytes=60 * 1024 * 1024),
        )(x_rows, w_x1, w_h1, w_x2, w_h2, b_1, b_2[None], h_zero, c_wide)
        return out, c_out[:, :, ::4]

    return jax.shard_map(local, mesh=mesh,
                         in_specs=(spec_seq, spec_weight, spec_weight, P(None, 'col'), spec_weight,
                                   P('row', 'col'), P('col'), spec_seq, spec_seq),
                         out_specs=(spec_out, spec_out), check_vma=False)
```

time: 2580 us -> 395 us (0.15)
  waiting for transfers between devices: 1070 us -> 0.01 us
  blocking collectives: 918 us -> 0 us
  matrix products: 420 us -> 0 us
  Pallas kernels: 0 us -> 385 us
  local copies, waits for them, and re-layouts: 90.7 us -> 9.21 us
  other arithmetic: 60 us -> 0 us
    reduce_scatter x48 -> x0, waiting for transfers between devices: 1070 us -> none  [one_step(): lax.psum_scatter(part_z, 'row', scatter_dimension=1, tiled=True) + gate_bias]
    all_gather x96 -> x0, blocking collectives: 918 us -> none  [the longest x48 667 us: one_step(): h_full = lax.all_gather(h_cols, 'col', axis=1, tiled=True)]
    dot_general x96 -> x0, matrix products: 420 us -> none  [the longest x48 307 us: one_step(): jnp.dot(in_t, w_in, preferred_element_type=jnp.float32)]
    pallas_call x0 -> x1, Pallas kernels: none -> 385 us  [local(): pl.pallas_call(functools.partial(lstm_kernel, steps, n_row, n_col), out_s...]
    add x48 -> x0, other arithmetic: 43.9 us -> none  [one_step(): lax.psum_scatter(part_z, 'row', scatter_dimension=1, tiled=True) + gate_bias]
    while x352 -> x0, local copies, waits for them, and re-layouts: 38 us -> none
  transfers between devices with their start and end apart: 49 -> 1, of which waited for: 48 -> 0; matrix products, arithmetic and copies ran while one was open for 1% -> 0% of each run, Pallas kernels for 0% -> 0%
where the time goes in v1:
time: 395 us
  Pallas kernels  385 us (97%)
  local copies, waits for them, and re-layouts  9.21 us (2%)
    pallas_call x1, Pallas kernels, local(): pl.pallas_call(functools.partial(lstm_kernel, steps, n_row, n_col), out_s...  385 us
  transfers between devices with their start and end apart: 1, of which 0 were waited for; matrix products, arithmetic and copies ran while one was open for 0% of the time, Pallas kernels for 0%

profile of v1, /device:TPU:0, one launch (start us, length us, event | category | flops | bytes accessed | tf_op | source)
XLA Modules:
  0.0 395.1 jit_solution(15561912949201881729)
XLA Ops:
  0.6 0.0 copy-start
  0.6 1.0 copy-done
  1.6 0.7 collective-permute-start
  2.3 0.0 collective-permute-done
  2.3 0.2 copy.11
  2.5 0.3 broadcast_in_dim.7
  2.8 1.2 copy.12.c0_ref
  4.0 384.5 %shard_map.104 = (bf16[16,32,256]{2,1,0:T(8,128)(2,1)}, f32[3,32,1024]{2,1,0:T(8,128)}) custom-call(bf16[16,32,1024]{2,1,0:T(8,128)(2,1)} %x_ref.1, bf16[2,1024,4096]{2,1,0:T(8,128)(2,1)} %wx1_hbm.1, bf16[2,1024,4096]{2,1,0:T(8,128)(2,1)} %wh1_hbm.1, bf16[2,1024,4096]{2,1,0:T(8,128)(2,1)} %wx2_hbm.1, bf16[1024,4096]{1,0:T(8,128)(2,1)} %wh2_hbm.1, ...), custom_call_target="tpu_custom_call" | custom-call | tf_op jit(solution)/shard_map/pallas_call | solution.py:261
  388.5 4.9 %slice.3 = f32[3,32,256]{2,1,0:T(8,128)} slice(f32[3,32,1024]{2,1,0:T(8,128)} %get-tuple-element.5), slice={[0:3:1], [0:32:1], [0:1024:4]} | slice | bytes 196608 | tf_op jit(solution)/shard_map/slice | solution.py:284
  393.4 1.7 copy.14
  (1 shorter events, 0.0 us)
Async XLA Ops:
  0.6 1.0 copy-start
  1.6 0.7 collective-permute-start

commit v2 on v1

--- a/solution.py
+++ b/solution.py
@@ -15,9 +15,9 @@
 
 def lstm_kernel(steps, n_row, n_col,
                 x_ref, wx1_hbm, wh1_hbm, wx2_hbm, wh2_hbm, b1_ref, b2_ref, h0_ref, c0_ref,
-                out_ref, c_ref,
-                wx, wh, wh2, hist, h2b, zp, p1r, yr, hsend, sel,
-                w_sem, p1_send, p1_recv, y_send, y_recv, h_send, h_recv):
+                out_ref, c_out,
+                wx, wh, wh2, hist, h2b, zp, p1r, yr, hsend, sel, spread, c_own, c_ref,
+                c_sem, w_sem, p1_send, p1_recv, y_send, y_recv, h_send, h_recv):
     row = lax.axis_index('row')
     col = lax.axis_index('col')
     batch, d_row = x_ref.shape[1], x_ref.shape[2]
@@ -65,10 +65,35 @@
             hist[k, 0, j] = h0_ref[k, :, j * unit_n:(j + 1) * unit_n].astype(BF16)
     for j in range(n_row):
         h2b[0, j] = h0_ref[2, :, j * unit_n:(j + 1) * unit_n].astype(BF16)
-    c_ref[...] = c0_ref[...]
+    rr = lax.broadcasted_iota(jnp.int32, (unit_n, width), 0)
+    cc = lax.broadcasted_iota(jnp.int32, (unit_n, width), 1)
+    spread[...] = jnp.where(rr == cc // 4, 1.0, 0.0).astype(BF16)
+
+    own_stays = row == col
+    c_part = pl.ds(pl.multiple_of(col * unit_n, LANES), unit_n)
+    c_copy = pltpu.make_async_remote_copy(
+        src_ref=c0_ref.at[:, :, c_part], dst_ref=c_own, send_sem=c_sem.at[0], recv_sem=c_sem.at[1],
+        device_id={'col': row, 'row': col}, device_id_type=MESH)
+    pl.semaphore_wait(barrier, n_col * n_row - 1)
+
+    @pl.when(jnp.logical_not(own_stays))
+    def _():
+        c_copy.start()
+
+    @pl.when(own_stays)
+    def _():
+        c_own[...] = c0_ref[:, :, c_part]
 
     def dot(a, w):
         return jnp.dot(a, w, preferred_element_type=F32)
+
+    def moved(a, m):
+        a = a * 0.5
+        top = a.astype(BF16)
+        rest = a - top.astype(F32)
+        mid = rest.astype(BF16)
+        low = (rest - mid.astype(F32)).astype(BF16)
+        return (dot(top, m) + dot(mid, m) + dot(low, m)) * 2.0
 
     def joined(blocks):
         return jnp.concatenate([blocks[j] for j in range(n_row)], axis=1)
@@ -84,7 +109,12 @@
     input_product(1, steps - 1)
     load_wait('h0')
     load_wait('h1')
-    pl.semaphore_wait(barrier, n_col * n_row - 1)
+
+    @pl.when(jnp.logical_not(own_stays))
+    def _():
+        c_copy.wait()
+    for k in range(3):
+        c_ref[k] = moved(c_own[k], spread[...])
 
     def mate_copy(k, slot, part):
         return pltpu.make_async_remote_copy(
@@ -103,8 +133,6 @@
             src_ref=hsend.at[k], dst_ref=dst.at[row],
             send_sem=h_send.at[k, i], recv_sem=h_recv.at[k, slot, row],
             device_id={'col': (col + i) % n_col, 'row': col}, device_id_type=MESH)
-
-    own_stays = row == col
 
     def h_start(k, dst, slot):
         for i in range(n_col - 1, 0, -1):
@@ -236,6 +264,8 @@
         return carry
 
     lax.fori_loop(0, steps, layer_two, 0)
+    for k in range(3):
+        c_out[k] = moved(c_ref[k], sel[...])
 
 
 def solution(mesh):
@@ -246,22 +276,16 @@
     spec_out = P(None, 'data', ('col', 'row'))
 
     def local(x_rows, w_x1, w_h1, b_1, w_x2, w_h2, b_2, h_zero, c_zero):
-        row_idx = lax.axis_index('row')
-        col_idx = lax.axis_index('col')
         steps, batch, d_row = x_rows.shape
         unit_n = d_row // n_col
         width = 4 * unit_n
-        c_part = lax.dynamic_slice_in_dim(c_zero, col_idx * unit_n, unit_n, axis=2)
-        pairs = [(b * n_row + a, a * n_row + b) for a in range(n_row) for b in range(n_col)]
-        c_own = lax.ppermute(c_part, ('col', 'row'), pairs)
-        c_wide = jnp.repeat(c_own, 4, axis=2)
         vmem = pl.BlockSpec(memory_space=pltpu.VMEM)
         hbm = pl.BlockSpec(memory_space=pl.ANY)
         dma = pltpu.SemaphoreType.DMA
-        out, c_out = pl.pallas_call(
+        return pl.pallas_call(
             functools.partial(lstm_kernel, steps, n_row, n_col),
             out_shape=(jax.ShapeDtypeStruct((steps, batch, unit_n), BF16),
-                       jax.ShapeDtypeStruct((3, batch, width), F32)),
+                       jax.ShapeDtypeStruct((3, batch, unit_n), F32)),
             in_specs=[vmem, hbm, hbm, hbm, hbm, vmem, vmem, vmem, vmem],
             out_specs=(vmem, vmem),
             scratch_shapes=[
@@ -275,13 +299,16 @@
                 pltpu.VMEM((2, 2, batch, width), F32),
                 pltpu.VMEM((3, batch, unit_n), BF16),
                 pltpu.VMEM((width, unit_n), BF16),
+                pltpu.VMEM((unit_n, width), BF16),
+                pltpu.VMEM((3, batch, unit_n), F32),
+                pltpu.VMEM((3, batch, width), F32),
+                dma((2,)),
                 dma((7, 4)), dma((2, 2)), dma((2, 2, 2)), dma((2,)), dma((2, 2)),
                 dma((3, n_col)), dma((3, 2, n_row)),
             ],
             compiler_params=pltpu.CompilerParams(
                 collective_id=0, has_side_effects=True, vmem_limit_bytes=60 * 1024 * 1024),
-        )(x_rows, w_x1, w_h1, w_x2, w_h2, b_1, b_2[None], h_zero, c_wide)
-        return out, c_out[:, :, ::4]
+        )(x_rows, w_x1, w_h1, w_x2, w_h2, b_1, b_2[None], h_zero, c_zero)
 
     return jax.shard_map(local, mesh=mesh,
                          in_specs=(spec_seq, spec_weight, spec_weight, P(None, 'col'), spec_weight,

time: 395 us -> 382 us (0.967)
  Pallas kernels: 385 us -> 378 us
  local copies, waits for them, and re-layouts: 9.21 us -> 3.21 us
    pallas_call x1, Pallas kernels: 385 us -> 378 us  [local(): pl.pallas_call(functools.partial(lstm_kernel, steps, n_row, n_col), out_s...]
    slice x1 -> x0, local copies, waits for them, and re-layouts: 4.91 us -> none  [local(): return (out, c_out[:, :, ::4])]
  transfers between devices with their start and end apart: 1 -> 0, of which waited for: 0 -> 0; matrix products, arithmetic and copies ran while one was open for 0% -> 0% of each run, Pallas kernels for 0% -> 0%
where the time goes in v2:
time: 382 us; the launch traced here: 381 us
  Pallas kernels  378 us (99%)
    pallas_call x1, Pallas kernels, local(): pl.pallas_call(functools.partial(lstm_kernel, steps, n_row, n_col), out_s...  378 us

profile of v2, /device:TPU:0, one launch (start us, length us, event | category | flops | bytes accessed | tf_op | source)
XLA Modules:
  0.0 381.4 jit_solution(13082028275193780648)
XLA Ops:
  0.6 377.5 %shard_map.104 = (bf16[16,32,256]{2,1,0:T(8,128)(2,1)}, f32[3,32,256]{2,1,0:T(8,128)}) custom-call(bf16[16,32,1024]{2,1,0:T(8,128)(2,1)} %x_ref.1, bf16[2,1024,4096]{2,1,0:T(8,128)(2,1)} %wx1_hbm.1, bf16[2,1024,4096]{2,1,0:T(8,128)(2,1)} %wh1_hbm.1, bf16[2,1024,4096]{2,1,0:T(8,128)(2,1)} %wx2_hbm.1, bf16[1024,4096]{1,0:T(8,128)(2,1)} %wh2_hbm.1, ...), custom_call_target="tpu_custom_call" | custom-call | tf_op jit(solution)/shard_map/pallas_call | solution.py:285
  378.2 1.7 copy.13
  379.8 1.5 copy.14

commit v3 on v2

--- a/solution.py
+++ b/solution.py
@@ -13,11 +13,13 @@
 LANES = 128
 
 
-def lstm_kernel(steps, n_row, n_col,
+def lstm_kernel(steps, n_data, n_row, n_col,
                 x_ref, wx1_hbm, wh1_hbm, wx2_hbm, wh2_hbm, b1_ref, b2_ref, h0_ref, c0_ref,
                 out_ref, c_out,
-                wx, wh, wh2, hist, h2b, zp, p1r, yr, hsend, sel, spread, c_own, c_ref,
-                c_sem, w_sem, p1_send, p1_recv, y_send, y_recv, h_send, h_recv):
+                wx, wh, wh2, hist, h2b, zp, p1r, yr, zm, m1r, myr, hsend, sel, spread, c_own, c_ref,
+                c_sem, w_sem, p1_send, p1_recv, y_send, y_recv, m1_send, m1_recv, my_send, my_recv,
+                h_send, h_recv, h2_send, h2_recv, h0_sem, move_send, move_recv, relay_send, relay_recv):
+    data = lax.axis_index('data')
     row = lax.axis_index('row')
     col = lax.axis_index('col')
     batch, d_row = x_ref.shape[1], x_ref.shape[2]
@@ -34,8 +36,7 @@
 
     loads = {'x0': (wx1_hbm.at[0], wx.at[0], 0), 'h0': (wh1_hbm.at[0], wh.at[0], 1),
              'x1': (wx1_hbm.at[1], wx.at[1], 2), 'h1': (wh1_hbm.at[1], wh.at[1], 3),
-             'h2': (wh2_hbm, wh2, 4),
-             'm0': (wx2_hbm.at[0], wx.at[0], 5), 'm1': (wx2_hbm.at[1], wx.at[1], 6)}
+             'm0': (wx2_hbm.at[0], wx.at[0], 4), 'm1': (wx2_hbm.at[1], wx.at[1], 5)}
 
     def load_start(name):
         for idx in range(4):
@@ -47,8 +48,36 @@
             src, dst, sem = loads[name]
             weight_copy(src, dst, idx, sem).wait()
 
-    for name in ('x0', 'h0', 'x1', 'h1', 'h2'):
+    for name in ('x0', 'h0', 'x1', 'h1'):
         load_start(name)
+
+    half = d_row // 2
+    piece = half // (2 * steps)
+    own_cols = pl.ds(pl.multiple_of(row // 2 * (2 * width), LANES), 2 * width)
+    far_cols = pl.ds(pl.multiple_of((1 - row // 2) * (2 * width), LANES), 2 * width)
+    h2_load = pltpu.make_async_copy(wh2_hbm.at[:, own_cols], wh2.at[0], w_sem.at[6, 0])
+    h2_load.start()
+
+    def piece_rows(part, p):
+        return pl.ds(pl.multiple_of(part * half + p * piece, 16), piece)
+
+    def move_copy(p):
+        rows = piece_rows(data, p)
+        return pltpu.make_async_remote_copy(
+            src_ref=wh2_hbm.at[rows, far_cols], dst_ref=wh2.at[1, rows],
+            send_sem=move_send, recv_sem=move_recv.at[p % 8],
+            device_id={'row': across}, device_id_type=MESH)
+
+    def relay_copy(p):
+        rows = piece_rows(data, p)
+        return pltpu.make_async_remote_copy(
+            src_ref=wh2.at[1, rows], dst_ref=wh2.at[1, rows],
+            send_sem=relay_send, recv_sem=relay_recv,
+            device_id={'data': 1 - data}, device_id_type=MESH)
+
+    def forward(p):
+        move_copy(p).wait_recv()
+        relay_copy(p).start()
 
     barrier = pltpu.get_barrier_semaphore()
     for dc in range(n_col):
@@ -56,6 +85,7 @@
             if dc or dr:
                 pl.semaphore_signal(barrier, inc=1, device_id_type=MESH,
                                     device_id={'col': (col + dc) % n_col, 'row': (row + dr) % n_row})
+    pl.semaphore_signal(barrier, inc=1, device_id_type=MESH, device_id={'data': 1 - data})
 
     rr = lax.broadcasted_iota(jnp.int32, (width, unit_n), 0)
     cc = lax.broadcasted_iota(jnp.int32, (width, unit_n), 1)
@@ -64,7 +94,7 @@
         for j in range(n_row):
             hist[k, 0, j] = h0_ref[k, :, j * unit_n:(j + 1) * unit_n].astype(BF16)
     for j in range(n_row):
-        h2b[0, j] = h0_ref[2, :, j * unit_n:(j + 1) * unit_n].astype(BF16)
+        h2b[0, 0, j] = h0_ref[2, :, j * unit_n:(j + 1) * unit_n].astype(BF16)
     rr = lax.broadcasted_iota(jnp.int32, (unit_n, width), 0)
     cc = lax.broadcasted_iota(jnp.int32, (unit_n, width), 1)
     spread[...] = jnp.where(rr == cc // 4, 1.0, 0.0).astype(BF16)
@@ -74,7 +104,7 @@
     c_copy = pltpu.make_async_remote_copy(
         src_ref=c0_ref.at[:, :, c_part], dst_ref=c_own, send_sem=c_sem.at[0], recv_sem=c_sem.at[1],
         device_id={'col': row, 'row': col}, device_id_type=MESH)
-    pl.semaphore_wait(barrier, n_col * n_row - 1)
+    pl.semaphore_wait(barrier, n_col * n_row)
 
     @pl.when(jnp.logical_not(own_stays))
     def _():
@@ -83,6 +113,11 @@
     @pl.when(own_stays)
     def _():
         c_own[...] = c0_ref[:, :, c_part]
+
+    h0_copy = pltpu.make_async_remote_copy(
+        src_ref=h2b.at[0, 0], dst_ref=h2b.at[0, 1], send_sem=h0_sem.at[0], recv_sem=h0_sem.at[1],
+        device_id={'row': across}, device_id_type=MESH)
+    h0_copy.start()
 
     def dot(a, w):
         return jnp.dot(a, w, preferred_element_type=F32)
@@ -93,7 +128,8 @@
         rest = a - top.astype(F32)
         mid = rest.astype(BF16)
         low = (rest - mid.astype(F32)).astype(BF16)
-        return (dot(top, m) + dot(mid, m) + dot(low, m)) * 2.0
+        parts = dot(jnp.concatenate([top, mid, low], axis=0), m)
+        return ((parts[:batch] + parts[batch:2 * batch]) + parts[2 * batch:]) * 2.0
 
     def joined(blocks):
         return jnp.concatenate([blocks[j] for j in range(n_row)], axis=1)
@@ -175,17 +211,16 @@
         zp[k, 1] = zp[k, 1] + p1r[k, slot, 0]
         across_copy(k, slot).start()
 
-    def gates(k, slot, cell, bias_ref, bias_row):
-        mate_copy(k, slot, 1).wait_recv()
-        across_copy(k, slot).wait_recv()
+    def gates(cell, bias_ref, bias_row, addends):
         gate = lax.broadcasted_iota(jnp.int32, (batch, LANES), 1) % 4
         scale = jnp.where(gate == 2, 1.0, 0.5)
         shift = jnp.where(gate == 2, 0.0, 0.5)
         pieces = []
         for p in range(width // LANES):
             lanes = slice(p * LANES, (p + 1) * LANES)
-            bias = bias_ref[bias_row:bias_row + 1, pl.ds(pl.multiple_of(row * width, LANES) + p * LANES, LANES)]
-            z = zp[k, 3, :, lanes] + p1r[k, slot, 1, :, lanes] + yr[k, slot, :, lanes] + bias
+            z = bias_ref[bias_row:bias_row + 1, pl.ds(pl.multiple_of(row * width, LANES) + p * LANES, LANES)]
+            for a in addends:
+                z = z + a[:, lanes]
             act = jnp.tanh(z * scale) * scale + shift
             f = pltpu.roll(act, LANES - 1, 1)
             g = pltpu.roll(act, LANES - 2, 1)
@@ -193,7 +228,12 @@
             c_new = f * c_ref[cell, :, lanes] + act * g
             c_ref[cell, :, lanes] = c_new
             pieces.append((o * jnp.tanh(c_new)).astype(BF16))
-        h = dot(jnp.concatenate(pieces, axis=1), sel[...]).astype(BF16)
+        return dot(jnp.concatenate(pieces, axis=1), sel[...]).astype(BF16)
+
+    def gates_one(k, slot):
+        mate_copy(k, slot, 1).wait_recv()
+        across_copy(k, slot).wait_recv()
+        h = gates(k, b1_ref, k, (zp.at[k, 3], p1r.at[k, slot, 1], yr.at[k, slot]))
         for part in range(2):
             mate_copy(k, slot, part).wait_send()
         across_copy(k, slot).wait_send()
@@ -208,13 +248,18 @@
             head(k, slot, hist.at[k, n], wh.at[k])
             middle(k, slot)
         for k in range(2):
-            h = gates(k, slot, k, b1_ref, k)
+            h = gates_one(k, slot)
 
             @pl.when(n > 0)
             def _(k=k):
                 h_wait_send(k, hist.at[k, n], slot)
             hsend[k] = h
             h_start(k, hist.at[k, n + 1], (n + 1) % 2)
+            move_copy(2 * n + k).start()
+
+            @pl.when(n > 0)
+            def _(k=k):
+                forward(2 * n - 2 + k)
 
             @pl.when(n < steps - 1)
             def _(k=k):
@@ -227,48 +272,143 @@
 
     lax.fori_loop(0, steps, layer_one, 0)
 
+    def mid_mate_copy(slot, part):
+        return pltpu.make_async_remote_copy(
+            src_ref=zp.at[1, 2 * part], dst_ref=m1r.at[slot, part],
+            send_sem=m1_send.at[part], recv_sem=m1_recv.at[slot, part],
+            device_id={'row': mate}, device_id_type=MESH)
+
+    def mid_across_copy(slot):
+        return pltpu.make_async_remote_copy(
+            src_ref=zp.at[1, 1], dst_ref=myr.at[slot],
+            send_sem=my_send, recv_sem=my_recv.at[slot],
+            device_id={'row': across}, device_id_type=MESH)
+
+    def mid_wait_send():
+        for part in range(2):
+            mid_mate_copy(0, part).wait_send()
+        mid_across_copy(0).wait_send()
+
     def mid_product(t):
+        slot = t % 3
         a = joined(hist.at[0, t + 1])
         b = joined(hist.at[1, steps - t])
         for idx in range(4):
-            zp[0, idx] = dot(a, wx[0, idx]) + dot(b, wx[1, idx])
-
+            z = dot(a, wx[0, idx]) + dot(b, wx[1, idx])
+            if idx < 3:
+                zp[1, idx] = z
+            else:
+                zm[t % 2] = z
+            if idx % 2 == 0:
+                mid_mate_copy(slot, idx // 2).start()
+        mid_mate_copy(slot, 0).wait_recv()
+        zp[1, 1] = zp[1, 1] + m1r[slot, 0]
+        mid_across_copy(slot).start()
+
+    def h2_copy(slot, i, p):
+        return pltpu.make_async_remote_copy(
+            src_ref=hsend.at[2], dst_ref=h2b.at[slot, p, row],
+            send_sem=h2_send.at[i, p], recv_sem=h2_recv.at[slot, p, row],
+            device_id={'col': (col + i) % n_col, 'row': (col + 2 * p) % n_row}, device_id_type=MESH)
+
+    h2_stays = [row == (col + 2 * p) % n_row for p in range(2)]
+
+    def h2_start(slot):
+        for i in range(n_col - 1, -1, -1):
+            for p in range(2):
+                if i:
+                    h2_copy(slot, i, p).start()
+                else:
+                    pl.when(jnp.logical_not(h2_stays[p]))(lambda p=p: h2_copy(slot, 0, p).start())
+
+                    @pl.when(h2_stays[p])
+                    def _(p=p):
+                        h2b[slot, p, row] = hsend[2]
+
+    def h2_wait_send(slot):
+        for i in range(n_col):
+            for p in range(2):
+                if i:
+                    h2_copy(slot, i, p).wait_send()
+                else:
+                    pl.when(jnp.logical_not(h2_stays[p]))(lambda p=p: h2_copy(slot, 0, p).wait_send())
+
+    def h2_wait_recv(slot):
+        for p in range(2):
+            for j in range(n_row):
+                def wait(p=p, j=j):
+                    pltpu.make_async_remote_copy(
+                        src_ref=hsend.at[2], dst_ref=h2b.at[slot, p, j],
+                        send_sem=h2_send.at[0, 0], recv_sem=h2_recv.at[slot, p, j],
+                        device_id={'col': col, 'row': row}, device_id_type=MESH).wait_recv()
+                pl.when(jnp.logical_not(h2_stays[p] & (row == j)))(wait)
+
+    for k in range(2):
+        forward(2 * steps - 2 + k)
     for k in range(2):
         h_wait_send(k, hist.at[k, steps], steps % 2)
-    for name in ('h2', 'm0', 'm1'):
+    for name in ('m0', 'm1'):
         load_wait(name)
+    mid_product(1)
     for k in range(2):
         h_wait_recv(k, hist.at[k, steps], steps % 2)
+    mid_wait_send()
     mid_product(0)
+    h2_load.wait()
+    h0_copy.wait()
+    moved_rows = wh2.at[1, pl.ds(pl.multiple_of(data * half, 16), half)]
+    came_rows = wh2.at[1, pl.ds(pl.multiple_of((1 - data) * half, 16), half)]
+    pltpu.make_async_remote_copy(
+        src_ref=moved_rows, dst_ref=moved_rows, send_sem=move_send, recv_sem=move_recv.at[0],
+        device_id={'row': across}, device_id_type=MESH).wait_send()
+    pltpu.make_async_remote_copy(
+        src_ref=moved_rows, dst_ref=came_rows, send_sem=relay_send, recv_sem=relay_recv,
+        device_id={'data': 1 - data}, device_id_type=MESH).wait()
 
     def layer_two(n, carry):
         slot = n % 2
 
         @pl.when(n > 0)
         def _():
-            h_wait_recv(2, h2b.at[slot], slot)
-        head(0, slot, h2b.at[slot], wh2)
-        middle(0, slot)
-        h = gates(0, slot, 2, b2_ref, 0)
+            h2_wait_recv(slot)
+        a = [joined(h2b.at[slot, p]) for p in range(2)]
+        for idx, part in ((0, 1 - core), (3, core)):
+            cols = pl.ds(pl.multiple_of(part * width, LANES), width)
+            zp[0, idx] = dot(a[0], wh2[0, :, cols]) + dot(a[1], wh2[1, :, cols])
+            if idx == 0:
+                mate_copy(0, slot, 0).start()
+        mate_copy(0, slot, 0).wait_recv()
+        mid_slot = n % 3
+        mid_mate_copy(mid_slot, 1).wait_recv()
+        mid_across_copy(mid_slot).wait_recv()
+        h = gates(2, b2_ref, 0, (zp.at[0, 3], p1r.at[0, slot, 0], zm.at[slot],
+                                 m1r.at[mid_slot, 1], myr.at[mid_slot]))
+        mate_copy(0, slot, 0).wait_send()
 
         @pl.when(n > 0)
         def _():
-            h_wait_send(2, h2b.at[slot], slot)
+            h2_wait_send(slot)
         hsend[2] = h
         out_ref[n] = h
 
         @pl.when(n < steps - 1)
         def _():
-            h_start(2, h2b.at[1 - slot], 1 - slot)
-            mid_product(n + 1)
+            h2_start(1 - slot)
+
+        @pl.when(n < steps - 2)
+        def _():
+            mid_wait_send()
+            mid_product(n + 2)
         return carry
 
     lax.fori_loop(0, steps, layer_two, 0)
+    mid_wait_send()
     for k in range(3):
         c_out[k] = moved(c_ref[k], sel[...])
 
 
 def solution(mesh):
+    n_data = mesh.shape['data']
     n_row = mesh.shape['row']
     n_col = mesh.shape['col']
     spec_seq = P(None, 'data', 'row')
@@ -283,7 +423,7 @@
         hbm = pl.BlockSpec(memory_space=pl.ANY)
         dma = pltpu.SemaphoreType.DMA
         return pl.pallas_call(
-            functools.partial(lstm_kernel, steps, n_row, n_col),
+            functools.partial(lstm_kernel, steps, n_data, n_row, n_col),
             out_shape=(jax.ShapeDtypeStruct((steps, batch, unit_n), BF16),
                        jax.ShapeDtypeStruct((3, batch, unit_n), F32)),
             in_specs=[vmem, hbm, hbm, hbm, hbm, vmem, vmem, vmem, vmem],
@@ -291,12 +431,15 @@
             scratch_shapes=[
                 pltpu.VMEM((2, 4, d_row, width), BF16),
                 pltpu.VMEM((2, 4, d_row, width), BF16),
-                pltpu.VMEM((4, d_row, width), BF16),
+                pltpu.VMEM((2, d_row, 2 * width), BF16),
                 pltpu.VMEM((2, steps + 1, n_row, batch, unit_n), BF16),
-                pltpu.VMEM((2, n_row, batch, unit_n), BF16),
+                pltpu.VMEM((2, 2, n_row, batch, unit_n), BF16),
                 pltpu.VMEM((2, 4, batch, width), F32),
                 pltpu.VMEM((2, 2, 2, batch, width), F32),
                 pltpu.VMEM((2, 2, batch, width), F32),
+                pltpu.VMEM((2, batch, width), F32),
+                pltpu.VMEM((3, 2, batch, width), F32),
+                pltpu.VMEM((3, batch, width), F32),
                 pltpu.VMEM((3, batch, unit_n), BF16),
                 pltpu.VMEM((width, unit_n), BF16),
                 pltpu.VMEM((unit_n, width), BF16),
@@ -304,7 +447,9 @@
                 pltpu.VMEM((3, batch, width), F32),
                 dma((2,)),
                 dma((7, 4)), dma((2, 2)), dma((2, 2, 2)), dma((2,)), dma((2, 2)),
-                dma((3, n_col)), dma((3, 2, n_row)),
+                dma((2,)), dma((3, 2)), dma, dma((3,)),
+                dma((2, n_col)), dma((2, 2, n_row)), dma((n_col, 2)), dma((2, 2, n_row)),
+                dma((2,)), dma, dma((8,)), dma, dma,
             ],
             compiler_params=pltpu.CompilerParams(
                 collective_id=0, has_side_effects=True, vmem_limit_bytes=60 * 1024 * 1024),

time: 382 us -> 352 us (0.921)
  Pallas kernels: 378 us -> 348 us
    pallas_call x1, Pallas kernels: 378 us -> 348 us  [local(): pl.pallas_call(functools.partial(lstm_kernel, steps, n_data, n_row, n_col...]
where the time goes in v3:
time: 352 us
  Pallas kernels  348 us (99%)
    pallas_call x1, Pallas kernels, local(): pl.pallas_call(functools.partial(lstm_kernel, steps, n_data, n_row, n_col...  348 us

profile of v3, /device:TPU:0, one launch (start us, length us, event | category | flops | bytes accessed | tf_op | source)
XLA Modules:
  0.0 351.5 jit_solution(16300166812565626837)
XLA Ops:
  0.6 347.7 %shard_map.104 = (bf16[16,32,256]{2,1,0:T(8,128)(2,1)}, f32[3,32,256]{2,1,0:T(8,128)}) custom-call(bf16[16,32,1024]{2,1,0:T(8,128)(2,1)} %x_ref.1, bf16[2,1024,4096]{2,1,0:T(8,128)(2,1)} %wx1_hbm.1, bf16[2,1024,4096]{2,1,0:T(8,128)(2,1)} %wh1_hbm.1, bf16[2,1024,4096]{2,1,0:T(8,128)(2,1)} %wx2_hbm.1, bf16[1024,4096]{1,0:T(8,128)(2,1)} %wh2_hbm.1, ...), custom_call_target="tpu_custom_call" | custom-call | tf_op jit(solution)/shard_map/pallas_call | solution.py:425
  348.3 1.7 copy.13
  350.0 1.5 copy.14

commit v4 on v3

--- a/solution.py
+++ b/solution.py
@@ -11,6 +11,7 @@
 F32 = jnp.float32
 BF16 = jnp.bfloat16
 LANES = 128
+SPLIT = 2
 
 
 def lstm_kernel(steps, n_data, n_row, n_col,
@@ -25,6 +26,7 @@
     batch, d_row = x_ref.shape[1], x_ref.shape[2]
     unit_n = d_row // n_col
     width = 4 * unit_n
+    part_n = width // SPLIT
     core = row % 2
     mate = row + 1 - 2 * core
     across = (row + 2) % 4
@@ -122,6 +124,9 @@
     def dot(a, w):
         return jnp.dot(a, w, preferred_element_type=F32)
 
+    def lanes_of(s):
+        return slice(s * part_n, (s + 1) * part_n)
+
     def moved(a, m):
         a = a * 0.5
         top = a.astype(BF16)
@@ -137,7 +142,8 @@
     def input_product(k, t):
         a = x_ref[t]
         for idx in range(4):
-            zp[k, idx] = dot(a, wx[k, idx])
+            for s in range(SPLIT):
+                zp[k, idx, s] = dot(a, wx[k, idx, :, lanes_of(s)])
 
     load_wait('x0')
     input_product(0, 0)
@@ -152,43 +158,38 @@
     for k in range(3):
         c_ref[k] = moved(c_own[k], spread[...])
 
-    def mate_copy(k, slot, part):
-        return pltpu.make_async_remote_copy(
-            src_ref=zp.at[k, 2 * part], dst_ref=p1r.at[k, slot, part],
-            send_sem=p1_send.at[k, part], recv_sem=p1_recv.at[k, slot, part],
+    def mate_copy(k, slot, part, s):
+        return pltpu.make_async_remote_copy(
+            src_ref=zp.at[k, 2 * part, s], dst_ref=p1r.at[k, slot, part, s],
+            send_sem=p1_send.at[k, part, s], recv_sem=p1_recv.at[k, slot, part, s],
             device_id={'row': mate}, device_id_type=MESH)
 
-    def across_copy(k, slot):
-        return pltpu.make_async_remote_copy(
-            src_ref=zp.at[k, 1], dst_ref=yr.at[k, slot],
-            send_sem=y_send.at[k], recv_sem=y_recv.at[k, slot],
+    def across_copy(k, slot, s):
+        return pltpu.make_async_remote_copy(
+            src_ref=zp.at[k, 1, s], dst_ref=yr.at[k, slot, s],
+            send_sem=y_send.at[k, s], recv_sem=y_recv.at[k, slot, s],
             device_id={'row': across}, device_id_type=MESH)
+
+    def far(i):
+        return (n_col - 1 - i) + (2 * i - (n_col - 1)) * (col // (n_col // 2))
 
     def h_copy(k, dst, slot, i):
         return pltpu.make_async_remote_copy(
             src_ref=hsend.at[k], dst_ref=dst.at[row],
             send_sem=h_send.at[k, i], recv_sem=h_recv.at[k, slot, row],
-            device_id={'col': (col + i) % n_col, 'row': col}, device_id_type=MESH)
+            device_id={'col': far(i), 'row': col}, device_id_type=MESH)
 
     def h_start(k, dst, slot):
-        for i in range(n_col - 1, 0, -1):
-            h_copy(k, dst, slot, i).start()
-
-        @pl.when(jnp.logical_not(own_stays))
-        def _():
-            h_copy(k, dst, slot, 0).start()
+        for i in range(n_col):
+            pl.when(jnp.logical_not(own_stays & (far(i) == col)))(lambda i=i: h_copy(k, dst, slot, i).start())
 
         @pl.when(own_stays)
         def _():
             dst[row] = hsend[k]
 
     def h_wait_send(k, dst, slot):
-        for i in range(1, n_col):
-            h_copy(k, dst, slot, i).wait_send()
-
-        @pl.when(jnp.logical_not(own_stays))
-        def _():
-            h_copy(k, dst, slot, 0).wait_send()
+        for i in range(n_col):
+            pl.when(jnp.logical_not(own_stays & (far(i) == col)))(lambda i=i: h_copy(k, dst, slot, i).wait_send())
 
     def h_wait_recv(k, dst, slot):
         for j in range(n_row):
@@ -201,15 +202,28 @@
 
     def head(k, slot, blocks, w_rec):
         a = joined(blocks)
+        todo = []
+
+        def finish(idx, s, z):
+            zp[k, idx, s] = zp[k, idx, s] + z
+            if idx % 2 == 0:
+                mate_copy(k, slot, idx // 2, s).start()
+
         for idx in range(4):
-            zp[k, idx] = zp[k, idx] + dot(a, w_rec[idx])
-            if idx % 2 == 0:
-                mate_copy(k, slot, idx // 2).start()
+            for s in range(SPLIT):
+                todo.append((idx, s, dot(a, w_rec[idx, :, lanes_of(s)])))
+                if len(todo) > 1:
+                    finish(*todo.pop(0))
+            if idx == 2:
+                finish(*todo.pop(0))
+                middle(k, slot)
+        finish(*todo.pop(0))
 
     def middle(k, slot):
-        mate_copy(k, slot, 0).wait_recv()
-        zp[k, 1] = zp[k, 1] + p1r[k, slot, 0]
-        across_copy(k, slot).start()
+        for s in range(SPLIT):
+            mate_copy(k, slot, 0, s).wait_recv()
+            zp[k, 1, s] = zp[k, 1, s] + p1r[k, slot, 0, s]
+            across_copy(k, slot, s).start()
 
     def gates(cell, bias_ref, bias_row, addends):
         gate = lax.broadcasted_iota(jnp.int32, (batch, LANES), 1) % 4
@@ -220,7 +234,7 @@
             lanes = slice(p * LANES, (p + 1) * LANES)
             z = bias_ref[bias_row:bias_row + 1, pl.ds(pl.multiple_of(row * width, LANES) + p * LANES, LANES)]
             for a in addends:
-                z = z + a[:, lanes]
+                z = z + a[p * LANES // part_n, :, pl.ds(p * LANES % part_n, LANES)]
             act = jnp.tanh(z * scale) * scale + shift
             f = pltpu.roll(act, LANES - 1, 1)
             g = pltpu.roll(act, LANES - 2, 1)
@@ -231,12 +245,14 @@
         return dot(jnp.concatenate(pieces, axis=1), sel[...]).astype(BF16)
 
     def gates_one(k, slot):
-        mate_copy(k, slot, 1).wait_recv()
-        across_copy(k, slot).wait_recv()
+        for s in range(SPLIT):
+            mate_copy(k, slot, 1, s).wait_recv()
+            across_copy(k, slot, s).wait_recv()
         h = gates(k, b1_ref, k, (zp.at[k, 3], p1r.at[k, slot, 1], yr.at[k, slot]))
-        for part in range(2):
-            mate_copy(k, slot, part).wait_send()
-        across_copy(k, slot).wait_send()
+        for s in range(SPLIT):
+            for part in range(2):
+                mate_copy(k, slot, part, s).wait_send()
+            across_copy(k, slot, s).wait_send()
         return h
 
     def layer_one(n, carry):
@@ -246,7 +262,6 @@
             def _(k=k):
                 h_wait_recv(k, hist.at[k, n], slot)
             head(k, slot, hist.at[k, n], wh.at[k])
-            middle(k, slot)
         for k in range(2):
             h = gates_one(k, slot)
 
@@ -255,11 +270,14 @@
                 h_wait_send(k, hist.at[k, n], slot)
             hsend[k] = h
             h_start(k, hist.at[k, n + 1], (n + 1) % 2)
-            move_copy(2 * n + k).start()
 
             @pl.when(n > 0)
             def _(k=k):
                 forward(2 * n - 2 + k)
+
+            if k == 1:
+                move_copy(2 * n).start()
+                move_copy(2 * n + 1).start()
 
             @pl.when(n < steps - 1)
             def _(k=k):
@@ -294,11 +312,12 @@
         a = joined(hist.at[0, t + 1])
         b = joined(hist.at[1, steps - t])
         for idx in range(4):
-            z = dot(a, wx[0, idx]) + dot(b, wx[1, idx])
-            if idx < 3:
-                zp[1, idx] = z
-            else:
-                zm[t % 2] = z
+            for s in range(SPLIT):
+                z = dot(a, wx[0, idx, :, lanes_of(s)]) + dot(b, wx[1, idx, :, lanes_of(s)])
+                if idx < 3:
+                    zp[1, idx, s] = z
+                else:
+                    zm[t % 2, s] = z
             if idx % 2 == 0:
                 mid_mate_copy(slot, idx // 2).start()
         mid_mate_copy(slot, 0).wait_recv()
@@ -309,29 +328,24 @@
         return pltpu.make_async_remote_copy(
             src_ref=hsend.at[2], dst_ref=h2b.at[slot, p, row],
             send_sem=h2_send.at[i, p], recv_sem=h2_recv.at[slot, p, row],
-            device_id={'col': (col + i) % n_col, 'row': (col + 2 * p) % n_row}, device_id_type=MESH)
+            device_id={'col': far(i), 'row': (col + 2 * p) % n_row}, device_id_type=MESH)
 
     h2_stays = [row == (col + 2 * p) % n_row for p in range(2)]
 
     def h2_start(slot):
-        for i in range(n_col - 1, -1, -1):
+        for i in range(n_col):
             for p in range(2):
-                if i:
-                    h2_copy(slot, i, p).start()
-                else:
-                    pl.when(jnp.logical_not(h2_stays[p]))(lambda p=p: h2_copy(slot, 0, p).start())
-
-                    @pl.when(h2_stays[p])
-                    def _(p=p):
-                        h2b[slot, p, row] = hsend[2]
+                pl.when(jnp.logical_not(h2_stays[p] & (far(i) == col)))(lambda i=i, p=p: h2_copy(slot, i, p).start())
+        for p in range(2):
+            @pl.when(h2_stays[p])
+            def _(p=p):
+                h2b[slot, p, row] = hsend[2]
 
     def h2_wait_send(slot):
         for i in range(n_col):
             for p in range(2):
-                if i:
-                    h2_copy(slot, i, p).wait_send()
-                else:
-                    pl.when(jnp.logical_not(h2_stays[p]))(lambda p=p: h2_copy(slot, 0, p).wait_send())
+                pl.when(jnp.logical_not(h2_stays[p] & (far(i) == col)))(
+                    lambda i=i, p=p: h2_copy(slot, i, p).wait_send())
 
     def h2_wait_recv(slot):
         for p in range(2):
@@ -372,18 +386,29 @@
         def _():
             h2_wait_recv(slot)
         a = [joined(h2b.at[slot, p]) for p in range(2)]
+        todo = []
+
+        def finish(idx, s, z):
+            zp[0, idx, s] = z
+            if idx == 0:
+                mate_copy(0, slot, 0, s).start()
+
         for idx, part in ((0, 1 - core), (3, core)):
-            cols = pl.ds(pl.multiple_of(part * width, LANES), width)
-            zp[0, idx] = dot(a[0], wh2[0, :, cols]) + dot(a[1], wh2[1, :, cols])
-            if idx == 0:
-                mate_copy(0, slot, 0).start()
-        mate_copy(0, slot, 0).wait_recv()
+            for s in range(SPLIT):
+                cols = pl.ds(pl.multiple_of(part * width + s * part_n, LANES), part_n)
+                todo.append((idx, s, dot(a[0], wh2[0, :, cols]) + dot(a[1], wh2[1, :, cols])))
+                if len(todo) > 1:
+                    finish(*todo.pop(0))
+        finish(*todo.pop(0))
+        for s in range(SPLIT):
+            mate_copy(0, slot, 0, s).wait_recv()
         mid_slot = n % 3
         mid_mate_copy(mid_slot, 1).wait_recv()
         mid_across_copy(mid_slot).wait_recv()
         h = gates(2, b2_ref, 0, (zp.at[0, 3], p1r.at[0, slot, 0], zm.at[slot],
                                  m1r.at[mid_slot, 1], myr.at[mid_slot]))
-        mate_copy(0, slot, 0).wait_send()
+        for s in range(SPLIT):
+            mate_copy(0, slot, 0, s).wait_send()
 
         @pl.when(n > 0)
         def _():
@@ -434,19 +459,19 @@
                 pltpu.VMEM((2, d_row, 2 * width), BF16),
                 pltpu.VMEM((2, steps + 1, n_row, batch, unit_n), BF16),
                 pltpu.VMEM((2, 2, n_row, batch, unit_n), BF16),
-                pltpu.VMEM((2, 4, batch, width), F32),
-                pltpu.VMEM((2, 2, 2, batch, width), F32),
-                pltpu.VMEM((2, 2, batch, width), F32),
-                pltpu.VMEM((2, batch, width), F32),
-                pltpu.VMEM((3, 2, batch, width), F32),
-                pltpu.VMEM((3, batch, width), F32),
+                pltpu.VMEM((2, 4, SPLIT, batch, width // SPLIT), F32),
+                pltpu.VMEM((2, 2, 2, SPLIT, batch, width // SPLIT), F32),
+                pltpu.VMEM((2, 2, SPLIT, batch, width // SPLIT), F32),
+                pltpu.VMEM((2, SPLIT, batch, width // SPLIT), F32),
+                pltpu.VMEM((3, 2, SPLIT, batch, width // SPLIT), F32),
+                pltpu.VMEM((3, SPLIT, batch, width // SPLIT), F32),
                 pltpu.VMEM((3, batch, unit_n), BF16),
                 pltpu.VMEM((width, unit_n), BF16),
                 pltpu.VMEM((unit_n, width), BF16),
                 pltpu.VMEM((3, batch, unit_n), F32),
                 pltpu.VMEM((3, batch, width), F32),
                 dma((2,)),
-                dma((7, 4)), dma((2, 2)), dma((2, 2, 2)), dma((2,)), dma((2, 2)),
+                dma((7, 4)), dma((2, 2, SPLIT)), dma((2, 2, 2, SPLIT)), dma((2, SPLIT)), dma((2, 2, SPLIT)),
                 dma((2,)), dma((3, 2)), dma, dma((3,)),
                 dma((2, n_col)), dma((2, 2, n_row)), dma((n_col, 2)), dma((2, 2, n_row)),
                 dma((2,)), dma, dma((8,)), dma, dma,

time: 352 us -> 335 us (0.952)
  Pallas kernels: 348 us -> 331 us
    pallas_call x1, Pallas kernels: 348 us -> 331 us  [local(): pl.pallas_call(functools.partial(lstm_kernel, steps, n_data, n_row, n_col...]
where the time goes in v4:
time: 335 us
  Pallas kernels  331 us (99%)
    pallas_call x1, Pallas kernels, local(): pl.pallas_call(functools.partial(lstm_kernel, steps, n_data, n_row, n_col...  331 us

profile of v4, /device:TPU:0, one launch (start us, length us, event | category | flops | bytes accessed | tf_op | source)
XLA Modules:
  0.0 334.7 jit_solution(10666951453515650206)
XLA Ops:
  0.6 330.9 %shard_map.104 = (bf16[16,32,256]{2,1,0:T(8,128)(2,1)}, f32[3,32,256]{2,1,0:T(8,128)}) custom-call(bf16[16,32,1024]{2,1,0:T(8,128)(2,1)} %x_ref.1, bf16[2,1024,4096]{2,1,0:T(8,128)(2,1)} %wx1_hbm.1, bf16[2,1024,4096]{2,1,0:T(8,128)(2,1)} %wh1_hbm.1, bf16[2,1024,4096]{2,1,0:T(8,128)(2,1)} %wx2_hbm.1, bf16[1024,4096]{1,0:T(8,128)(2,1)} %wh2_hbm.1, ...), custom_call_target="tpu_custom_call" | custom-call | tf_op jit(solution)/shard_map/pallas_call | solution.py:450
  331.5 1.7 copy.13
  333.2 1.5 copy.14

commit v5 on v4

--- a/solution.py
+++ b/solution.py
@@ -147,10 +147,7 @@
 
     load_wait('x0')
     input_product(0, 0)
-    load_wait('x1')
-    input_product(1, steps - 1)
     load_wait('h0')
-    load_wait('h1')
 
     @pl.when(jnp.logical_not(own_stays))
     def _():
@@ -216,8 +213,10 @@
                     finish(*todo.pop(0))
             if idx == 2:
                 finish(*todo.pop(0))
-                middle(k, slot)
+                pl.when(core == 0)(lambda: middle(k, slot))
         finish(*todo.pop(0))
+        if k:
+            pl.when(core != 0)(lambda: middle(k, slot))
 
     def middle(k, slot):
         for s in range(SPLIT):
@@ -258,6 +257,13 @@
     def layer_one(n, carry):
         slot = n % 2
         for k in range(2):
+            if k == 1:
+                pl.when(n == 0)(lambda: load_wait('x1'))
+                input_product(1, steps - 1 - n)
+                pl.when(core != 0)(lambda: middle(0, slot))
+                pl.when(n == 0)(lambda: load_wait('h1'))
+                pl.when(n == steps - 1)(lambda: load_start('m1'))
+
             @pl.when(n > 0)
             def _(k=k):
                 h_wait_recv(k, hist.at[k, n], slot)
@@ -275,17 +281,15 @@
             def _(k=k):
                 forward(2 * n - 2 + k)
 
-            if k == 1:
+            if k == 0:
                 move_copy(2 * n).start()
                 move_copy(2 * n + 1).start()
 
-            @pl.when(n < steps - 1)
-            def _(k=k):
-                input_product(k, n + 1 if k == 0 else steps - 2 - n)
-
-            @pl.when(n == steps - 1)
-            def _(k=k):
-                load_start('m0' if k == 0 else 'm1')
+            if k == 0:
+                @pl.when(n < steps - 1)
+                def _():
+                    input_product(0, n + 1)
+                pl.when(n == steps - 1)(lambda: load_start('m0'))
         return carry
 
     lax.fori_loop(0, steps, layer_one, 0)
@@ -347,15 +351,20 @@
                 pl.when(jnp.logical_not(h2_stays[p] & (far(i) == col)))(
                     lambda i=i, p=p: h2_copy(slot, i, p).wait_send())
 
-    def h2_wait_recv(slot):
-        for p in range(2):
-            for j in range(n_row):
-                def wait(p=p, j=j):
-                    pltpu.make_async_remote_copy(
-                        src_ref=hsend.at[2], dst_ref=h2b.at[slot, p, j],
-                        send_sem=h2_send.at[0, 0], recv_sem=h2_recv.at[slot, p, j],
-                        device_id={'col': col, 'row': row}, device_id_type=MESH).wait_recv()
-                pl.when(jnp.logical_not(h2_stays[p] & (row == j)))(wait)
+    def h2_wait_recv(slot, p):
+        stays = (row + 2 * p) % n_row == col
+        for j in range(n_row):
+            def wait(j=j):
+                pltpu.make_async_remote_copy(
+                    src_ref=hsend.at[2], dst_ref=h2b.at[slot, p, j],
+                    send_sem=h2_send.at[0, 0], recv_sem=h2_recv.at[slot, p, j],
+                    device_id={'col': col, 'row': row}, device_id_type=MESH).wait_recv()
+            pl.when(jnp.logical_not(stays & (row == j)))(wait)
+
+    def distance(r):
+        return (r - col) * (r - col)
+
+    nearer = jnp.where(distance(row) < distance((row + 2) % n_row), 0, 1)
 
     for k in range(2):
         forward(2 * steps - 2 + k)
@@ -382,21 +391,28 @@
     def layer_two(n, carry):
         slot = n % 2
 
-        @pl.when(n > 0)
-        def _():
-            h2_wait_recv(slot)
-        a = [joined(h2b.at[slot, p]) for p in range(2)]
+        parts = ((0, 1 - core), (3, core))
+
+        def cols_of(part, s):
+            return pl.ds(pl.multiple_of(part * width + s * part_n, LANES), part_n)
+
+        pl.when(n > 0)(lambda: h2_wait_recv(slot, nearer))
+        a = joined(h2b.at[slot, nearer])
+        for idx, part in parts:
+            for s in range(SPLIT):
+                zp[0, idx, s] = dot(a, wh2[nearer, :, cols_of(part, s)])
+        pl.when(n > 0)(lambda: h2_wait_recv(slot, 1 - nearer))
+        a = joined(h2b.at[slot, 1 - nearer])
         todo = []
 
         def finish(idx, s, z):
-            zp[0, idx, s] = z
+            zp[0, idx, s] = zp[0, idx, s] + z
             if idx == 0:
                 mate_copy(0, slot, 0, s).start()
 
-        for idx, part in ((0, 1 - core), (3, core)):
+        for idx, part in parts:
             for s in range(SPLIT):
-                cols = pl.ds(pl.multiple_of(part * width + s * part_n, LANES), part_n)
-                todo.append((idx, s, dot(a[0], wh2[0, :, cols]) + dot(a[1], wh2[1, :, cols])))
+                todo.append((idx, s, dot(a, wh2[1 - nearer, :, cols_of(part, s)])))
                 if len(todo) > 1:
                     finish(*todo.pop(0))
         finish(*todo.pop(0))

time: 335 us -> 320 us (0.955)
  Pallas kernels: 331 us -> 316 us
    pallas_call x1, Pallas kernels: 331 us -> 316 us  [local(): pl.pallas_call(functools.partial(lstm_kernel, steps, n_data, n_row, n_col...]
where the time goes in v5:
time: 320 us; the launch traced here: 319 us
  Pallas kernels  316 us (99%)
  local copies, waits for them, and re-layouts  3.21 us (1%)
    pallas_call x1, Pallas kernels, local(): pl.pallas_call(functools.partial(lstm_kernel, steps, n_data, n_row, n_col...  316 us

profile of v5, /device:TPU:0, one launch (start us, length us, event | category | flops | bytes accessed | tf_op | source)
XLA Modules:
  0.0 319.4 jit_solution(4015452827009784287)
XLA Ops:
  0.6 315.5 %shard_map.104 = (bf16[16,32,256]{2,1,0:T(8,128)(2,1)}, f32[3,32,256]{2,1,0:T(8,128)}) custom-call(bf16[16,32,1024]{2,1,0:T(8,128)(2,1)} %x_ref.1, bf16[2,1024,4096]{2,1,0:T(8,128)(2,1)} %wx1_hbm.1, bf16[2,1024,4096]{2,1,0:T(8,128)(2,1)} %wh1_hbm.1, bf16[2,1024,4096]{2,1,0:T(8,128)(2,1)} %wx2_hbm.1, bf16[1024,4096]{1,0:T(8,128)(2,1)} %wh2_hbm.1, ...), custom_call_target="tpu_custom_call" | custom-call | tf_op jit(solution)/shard_map/pallas_call | solution.py:466
  316.1 1.7 copy.13
  317.8 1.5 copy.14

commit v6 on v5

--- a/solution.py
+++ b/solution.py
@@ -336,10 +336,14 @@
 
     h2_stays = [row == (col + 2 * p) % n_row for p in range(2)]
 
+    cross = 1 - (col // 2 - row // 2) * (col // 2 - row // 2)
+
     def h2_start(slot):
         for i in range(n_col):
-            for p in range(2):
-                pl.when(jnp.logical_not(h2_stays[p] & (far(i) == col)))(lambda i=i, p=p: h2_copy(slot, i, p).start())
+            for q in range(2):
+                p = (q + cross) % 2
+                stays = (row == (col + 2 * p) % n_row) & (far(i) == col)
+                pl.when(jnp.logical_not(stays))(lambda i=i, p=p: h2_copy(slot, i, p).start())
         for p in range(2):
             @pl.when(h2_stays[p])
             def _(p=p):
@@ -463,7 +467,7 @@
         vmem = pl.BlockSpec(memory_space=pltpu.VMEM)
         hbm = pl.BlockSpec(memory_space=pl.ANY)
         dma = pltpu.SemaphoreType.DMA
-        return pl.pallas_call(
+        out = pl.pallas_call(
             functools.partial(lstm_kernel, steps, n_data, n_row, n_col),
             out_shape=(jax.ShapeDtypeStruct((steps, batch, unit_n), BF16),
                        jax.ShapeDtypeStruct((3, batch, unit_n), F32)),
@@ -496,6 +500,15 @@
                 collective_id=0, has_side_effects=True, vmem_limit_bytes=60 * 1024 * 1024),
         )(x_rows, w_x1, w_h1, w_x2, w_h2, b_1, b_2[None], h_zero, c_zero)
 
+        def copy_out(a_ref, b_ref, a_out, b_out):
+            a_out[...] = a_ref[...]
+            b_out[...] = b_ref[...]
+
+        return pl.pallas_call(
+            copy_out, in_specs=[vmem, vmem], out_specs=(vmem, vmem),
+            out_shape=(jax.ShapeDtypeStruct((steps, batch, unit_n), BF16),
+                       jax.ShapeDtypeStruct((3, batch, unit_n), F32)))(*out)
+
     return jax.shard_map(local, mesh=mesh,
                          in_specs=(spec_seq, spec_weight, spec_weight, P(None, 'col'), spec_weight,
                                    P('row', 'col'), P('col'), spec_seq, spec_seq),

time: 320 us -> 317 us (level)
  local copies, waits for them, and re-layouts: 3.21 us -> 0 us
    unnamed x2 -> x0, local copies, waits for them, and re-layouts: 3.21 us -> none
where the time goes in v6:
time: 317 us; the launch traced here: 316 us
  Pallas kernels  316 us (100%)
    pallas_call x1, Pallas kernels, local(): pl.pallas_call(functools.partial(lstm_kernel, steps, n_data, n_row, n_col...  314 us

profile of v6, /device:TPU:0, one launch (start us, length us, event | category | flops | bytes accessed | tf_op | source)
XLA Modules:
  0.0 316.4 jit_solution(2873287202978492628)
XLA Ops:
  0.6 314.1 %shard_map.104 = (bf16[16,32,256]{2,1,0:T(8,128)(2,1)}, f32[3,32,256]{2,1,0:T(8,128)}) custom-call(bf16[16,32,1024]{2,1,0:T(8,128)(2,1)} %x_ref.1, bf16[2,1024,4096]{2,1,0:T(8,128)(2,1)} %wx1_hbm.1, bf16[2,1024,4096]{2,1,0:T(8,128)(2,1)} %wh1_hbm.1, bf16[2,1024,4096]{2,1,0:T(8,128)(2,1)} %wx2_hbm.1, bf16[1024,4096]{1,0:T(8,128)(2,1)} %wh2_hbm.1, ...), custom_call_target="tpu_custom_call" | custom-call | tf_op jit(solution)/shard_map/pallas_call | solution.py:470
  314.7 1.7 shard_map.105

commit v7 on v6

--- a/solution.py
+++ b/solution.py
@@ -147,13 +147,13 @@
 
     load_wait('x0')
     input_product(0, 0)
-    load_wait('h0')
 
     @pl.when(jnp.logical_not(own_stays))
     def _():
         c_copy.wait()
     for k in range(3):
         c_ref[k] = moved(c_own[k], spread[...])
+    load_wait('h0')
 
     def mate_copy(k, slot, part, s):
         return pltpu.make_async_remote_copy(

time: 317 us -> 316 us (level)
  no operation moved by 1% of the time
where the time goes in v7:
time: 316 us
  Pallas kernels  315 us (100%)
    pallas_call x1, Pallas kernels, local(): pl.pallas_call(functools.partial(lstm_kernel, steps, n_data, n_row, n_col...  314 us

profile of v7, /device:TPU:0, one launch (start us, length us, event | category | flops | bytes accessed | tf_op | source)
XLA Modules:
  0.0 316.1 jit_solution(5671187019685967763)
XLA Ops:
  0.6 313.8 %shard_map.104 = (bf16[16,32,256]{2,1,0:T(8,128)(2,1)}, f32[3,32,256]{2,1,0:T(8,128)}) custom-call(bf16[16,32,1024]{2,1,0:T(8,128)(2,1)} %x_ref.1, bf16[2,1024,4096]{2,1,0:T(8,128)(2,1)} %wx1_hbm.1, bf16[2,1024,4096]{2,1,0:T(8,128)(2,1)} %wh1_hbm.1, bf16[2,1024,4096]{2,1,0:T(8,128)(2,1)} %wx2_hbm.1, bf16[1024,4096]{1,0:T(8,128)(2,1)} %wh2_hbm.1, ...), custom_call_target="tpu_custom_call" | custom-call | tf_op jit(solution)/shard_map/pallas_call | solution.py:470
  314.4 1.7 shard_map.105
